TPU v7x, 32 devices: a whole 2x2x4 slice. The times are simulated.
32 devices in a mesh: comp: 8 (over y, x, core), samp: 4 (over z).
Axes of the slice: x: 2, y: 2, z: 4, core: 2. Of those that a mesh axis runs over, the one named last changes fastest.
Arguments:
- start_points: float32 [512, 512], P('samp'), may hold values from -6 to 6
- centers: bfloat16 [65536, 512], P('comp'), may hold values from -1.25 to 1.25
- log_weights: float32 [65536], P('comp'), may hold values from -6 to 6
- noise_draws: bfloat16 [6, 512, 512], P(None, 'samp'), may hold values from -6 to 6
Outputs:
- final_points: float32 [512, 512], P('samp')
- log_mass: float32 [512], P('samp')
- occupancy: float32 [65536], P('comp')
All inputs are finite; a program needn't handle non-finite values.
Results may differ from a plain program's by a relative error of at most 0.0065.
Values sent between devices are 32-bit elements; how exact they have to be, the bound alone decides.
A program may use at most 128 MiB of HBM per device.

v0:
```python
import jax
import jax.numpy as jnp
from jax import lax
from jax.sharding import PartitionSpec as P

K = 65536
BLOCK = 2048
STEPS = 6


drift_rate = 0.5
noise_gain = 1.0


def joined(value, axis, join):
    pieces = jax.tree.map(lambda part: lax.all_gather(part, axis), value)
    head = jax.tree.map(lambda part: part[0], pieces)
    tail = jax.tree.map(lambda part: part[1:], pieces)
    so_far, _ = lax.scan(lambda so_far, section: (join(so_far, section), None), head, tail)
    return so_far


def combine_parts(earlier, later):
    top_one, mass_one, pull_one = earlier
    top_two, mass_two, pull_two = later
    top_new = jnp.maximum(top_one, top_two)
    scale_one = jnp.exp(top_one - top_new)
    scale_two = jnp.exp(top_two - top_new)
    return (
        top_new,
        scale_one * mass_one + scale_two * mass_two,
        scale_one[:, None] * pull_one + scale_two[:, None] * pull_two,
    )


def body(start_points, centers, log_weights, noise_draws):
    kdev = centers.shape[0]
    width = centers.shape[1]
    nblocks = kdev // BLOCK
    center_f = centers.astype(jnp.float32)
    bias_all = log_weights - 0.5 * jnp.sum(center_f * center_f, axis=1)
    center_blocks = centers.reshape(nblocks, BLOCK, width)
    bias_blocks = bias_all.reshape(nblocks, BLOCK)
    points = start_points
    occupancy_sum = jnp.zeros((kdev,), jnp.float32)
    log_mass = jnp.zeros((start_points.shape[0],), jnp.float32)
    for step_index in range(STEPS):
        points_bf = points.astype(jnp.bfloat16)

        def partial_block(pair):
            center_block, bias_block = pair
            scores = lax.dot_general(
                points_bf,
                center_block,
                (((1,), (1,)), ((), ())),
                preferred_element_type=jnp.float32,
            )
            scores = scores + bias_block[None, :]
            block_top = jnp.max(scores, axis=1)
            expd = jnp.exp(scores - block_top[:, None])
            block_mass = jnp.sum(expd, axis=1)
            pulled = jnp.dot(
                expd.astype(jnp.bfloat16), center_block, preferred_element_type=jnp.float32
            )
            return (scores, block_top, block_mass, pulled)

        all_scores, tops, masses, pulls = lax.map(partial_block, (center_blocks, bias_blocks))
        dev_top = jnp.max(tops, axis=0)
        factors = jnp.exp(tops - dev_top[None, :])
        dev_mass = jnp.sum(factors * masses, axis=0)
        dev_pull = jnp.sum(factors[:, :, None] * pulls, axis=0)
        noise_now = noise_draws[step_index]
        row_top, total_mass, total_pull = joined(
            (dev_top, dev_mass, dev_pull), "comp", combine_parts
        )
        points = (
            (1.0 - drift_rate) * points
            + drift_rate * (total_pull / total_mass[:, None])
            + noise_gain * noise_now.astype(jnp.float32)
        )
        log_mass = row_top + jnp.log(total_mass)
        shares = jnp.exp(all_scores - row_top[None, :, None]) / total_mass[None, :, None]
        occupancy_sum = occupancy_sum + jnp.sum(shares, axis=1).reshape(kdev)
    total_samples = start_points.shape[0] * lax.axis_size("samp")
    occupancy_all = lax.psum(occupancy_sum, "samp")
    occupancy = occupancy_all * (K / (total_samples * STEPS))
    return (points, log_mass, occupancy)


def solution(mesh):
    return jax.shard_map(
        body,
        mesh=mesh,
        in_specs=(P("samp", None), P("comp", None), P("comp"), P(None, "samp", None)),
        out_specs=(P("samp", None), P("samp"), P("comp")),
        check_vma=False,
    )
```

profile of v0, /device:TPU:0, one launch (start us, length us, event | category | flops | bytes accessed | tf_op | source)
XLA Modules:
  0.0 404.3 jit_solution(8402814084768957052)
XLA Ops:
  7.2 5.2 %multiply_reduce_fusion = f32[8192]{0:T(1024)S(1)} fusion(bf16[8192,512]{1,0:T(8,128)(2,1)} %param.29), kind=kLoop, calls=%fused_computation.168 | loop fusion | flops 12574720 | bytes 8421376 | tf_op jit(solution)/shard_map/reduce_sum | solution.py:41
  12.5 2.2 broadcast.66.clone
  14.9 24.3 %while.180 = (s32[]{:T(128)}, f32[4,128,2048]{1,2,0:T(8,128)}, f32[4,128]{1,0:T(4,128)S(1)}, f32[4,128]{1,0:T(4,128)S(1)}, f32[4,128,512]{2,1,0:T(8,128)S(1)}, /...) while((s32[]{:T(128)}, f32[4,128,2048]{1,2,0:T(8,128)}, ...), condition=%wide.region_4.5_spmd, body=%wide.region_1.4_spmd.sunk | while | flops 538443520 | bytes 9861245 | solution.py:67
  14.9 3.3 bitcast_dynamic-update-slice_fusion.12
  20.9 3.3 bitcast_dynamic-update-slice_fusion.12
  27.0 3.3 bitcast_dynamic-update-slice_fusion.12
  33.1 3.3 bitcast_dynamic-update-slice_fusion.12
  40.1 10.3 %all-gather.19 = f32[8,1,128]{2,1,0:T(1,128)S(1)} all-gather(f32[1,1,128]{2,1,0:T(1,128)S(1)} %bitcast.588), channel_id=3, replica_groups=mesh['comp'=8,'samp'=4] {'comp'}, dimensions={0}, use_global_device_ids=true | all-gather | bytes 4608 | tf_op jit(solution)/shard_map/all_gather | solution.py:16
  50.4 8.9 %all-gather.18 = f32[8,1,128]{2,1,0:T(1,128)S(1)} all-gather(f32[1,1,128]{2,1,0:T(1,128)S(1)} %bitcast.582), channel_id=2, replica_groups=mesh['comp'=8,'samp'=4] {'comp'}, dimensions={0}, use_global_device_ids=true | all-gather | bytes 4608 | tf_op jit(solution)/shard_map/all_gather | solution.py:16
  59.3 11.4 %all-gather.37.cloned.1.call-done = f32[1024,512]{1,0:T(8,128)} async-done(((f32[128,512]{1,0:T(8,128)}), f32[1024,512]{1,0:T(8,128)}) %all-gather.37.cloned.1.call-update) | async-done | bytes 2097168 | tf_op jit(solution)/shard_map/all_gather | solution.py:16
  74.7 2.2 broadcast.66.clone.1
  77.0 24.3 %while.182 = (s32[]{:T(128)}, f32[4,128,2048]{1,2,0:T(8,128)}, f32[4,128]{1,0:T(4,128)S(1)}, f32[4,128]{1,0:T(4,128)S(1)}, f32[4,128,512]{2,1,0:T(8,128)S(1)}, /...) while((s32[]{:T(128)}, f32[4,128,2048]{1,2,0:T(8,128)}, ...), condition=%wide.region_13.14_spmd, body=%wide.region_10.13_spmd.sunk | while | flops 538443520 | bytes 9861245 | solution.py:67
  77.0 3.3 bitcast_dynamic-update-slice_fusion.13
  83.1 3.3 bitcast_dynamic-update-slice_fusion.13
  86.7 2.1 fusion.220
  89.2 3.3 bitcast_dynamic-update-slice_fusion.13
  92.8 2.1 fusion.220
  95.3 3.3 bitcast_dynamic-update-slice_fusion.13
  102.3 8.7 %all-gather.21 = f32[8,1,128]{2,1,0:T(1,128)S(1)} all-gather(f32[1,1,128]{2,1,0:T(1,128)S(1)} %bitcast.589), channel_id=6, replica_groups=mesh['comp'=8,'samp'=4] {'comp'}, dimensions={0}, use_global_device_ids=true | all-gather | bytes 4608 | tf_op jit(solution)/shard_map/all_gather | solution.py:16
  111.0 7.9 %all-gather.20 = f32[8,1,128]{2,1,0:T(1,128)S(1)} all-gather(f32[1,1,128]{2,1,0:T(1,128)S(1)} %bitcast.583), channel_id=5, replica_groups=mesh['comp'=8,'samp'=4] {'comp'}, dimensions={0}, use_global_device_ids=true | all-gather | bytes 4608 | tf_op jit(solution)/shard_map/all_gather | solution.py:16
  119.0 11.2 %all-gather.39.cloned.1.call-done = f32[1024,512]{1,0:T(8,128)} async-done(((f32[128,512]{1,0:T(8,128)}), f32[1024,512]{1,0:T(8,128)}) %all-gather.39.cloned.1.call-update) | async-done | bytes 2097168 | tf_op jit(solution)/shard_map/all_gather | solution.py:16
  134.1 2.2 broadcast.66.clone.2
  136.5 24.3 %while.184 = (s32[]{:T(128)}, f32[4,128,2048]{1,2,0:T(8,128)}, f32[4,128]{1,0:T(4,128)S(1)}, f32[4,128]{1,0:T(4,128)S(1)}, f32[4,128,512]{2,1,0:T(8,128)S(1)}, /...) while((s32[]{:T(128)}, f32[4,128,2048]{1,2,0:T(8,128)}, ...), condition=%wide.region_22.23_spmd, body=%wide.region_19.22_spmd.sunk | while | flops 538443520 | bytes 9861245 | solution.py:67
  136.5 3.3 bitcast_dynamic-update-slice_fusion.14
  140.1 2.1 fusion.227
  142.6 3.3 bitcast_dynamic-update-slice_fusion.14
  148.7 3.3 bitcast_dynamic-update-slice_fusion.14
  154.7 3.3 bitcast_dynamic-update-slice_fusion.14
  158.3 2.1 fusion.227
  161.7 8.7 %all-gather.23 = f32[8,1,128]{2,1,0:T(1,128)S(1)} all-gather(f32[1,1,128]{2,1,0:T(1,128)S(1)} %bitcast.590), channel_id=9, replica_groups=mesh['comp'=8,'samp'=4] {'comp'}, dimensions={0}, use_global_device_ids=true | all-gather | bytes 4608 | tf_op jit(solution)/shard_map/all_gather | solution.py:16
  170.5 8.1 %all-gather.22 = f32[8,1,128]{2,1,0:T(1,128)S(1)} all-gather(f32[1,1,128]{2,1,0:T(1,128)S(1)} %bitcast.584), channel_id=8, replica_groups=mesh['comp'=8,'samp'=4] {'comp'}, dimensions={0}, use_global_device_ids=true | all-gather | bytes 4608 | tf_op jit(solution)/shard_map/all_gather | solution.py:16
  178.6 11.0 %all-gather.41.cloned.1.call-done = f32[1024,512]{1,0:T(8,128)} async-done(((f32[128,512]{1,0:T(8,128)}), f32[1024,512]{1,0:T(8,128)}) %all-gather.41.cloned.1.call-update) | async-done | bytes 2097168 | tf_op jit(solution)/shard_map/all_gather | solution.py:16
  193.5 2.2 broadcast.66.clone.3
  195.9 24.3 %while.186 = (s32[]{:T(128)}, f32[4,128,2048]{1,2,0:T(8,128)}, f32[4,128]{1,0:T(4,128)S(1)}, f32[4,128]{1,0:T(4,128)S(1)}, f32[4,128,512]{2,1,0:T(8,128)S(1)}, /...) while((s32[]{:T(128)}, f32[4,128,2048]{1,2,0:T(8,128)}, ...), condition=%wide.region_31.32_spmd, body=%wide.region_28.31_spmd.sunk | while | flops 538443520 | bytes 9861245 | solution.py:67
  196.0 3.4 bitcast_dynamic-update-slice_fusion.15
  202.1 3.3 bitcast_dynamic-update-slice_fusion.15
  208.2 3.3 bitcast_dynamic-update-slice_fusion.15
  214.2 3.3 bitcast_dynamic-update-slice_fusion.15
  221.2 8.7 %all-gather.25 = f32[8,1,128]{2,1,0:T(1,128)S(1)} all-gather(f32[1,1,128]{2,1,0:T(1,128)S(1)} %bitcast.591), channel_id=12, replica_groups=mesh['comp'=8,'samp'=4] {'comp'}, dimensions={0}, use_global_device_ids=true | all-gather | bytes 4608 | tf_op jit(solution)/shard_map/all_gather | solution.py:16
  230.0 7.9 %all-gather.24 = f32[8,1,128]{2,1,0:T(1,128)S(1)} all-gather(f32[1,1,128]{2,1,0:T(1,128)S(1)} %bitcast.585), channel_id=11, replica_groups=mesh['comp'=8,'samp'=4] {'comp'}, dimensions={0}, use_global_device_ids=true | all-gather | bytes 4608 | tf_op jit(solution)/shard_map/all_gather | solution.py:16
  237.9 11.2 %all-gather.43.cloned.1.call-done = f32[1024,512]{1,0:T(8,128)} async-done(((f32[128,512]{1,0:T(8,128)}), f32[1024,512]{1,0:T(8,128)}) %all-gather.43.cloned.1.call-update) | async-done | bytes 2097168 | tf_op jit(solution)/shard_map/all_gather | solution.py:16
  253.0 2.2 broadcast.66.clone.4
  255.4 24.3 %while.188 = (s32[]{:T(128)}, f32[4,128,2048]{1,2,0:T(8,128)}, f32[4,128]{1,0:T(4,128)S(1)}, f32[4,128]{1,0:T(4,128)S(1)}, f32[4,128,512]{2,1,0:T(8,128)S(1)}, /...) while((s32[]{:T(128)}, f32[4,128,2048]{1,2,0:T(8,128)}, ...), condition=%wide.region_40.41_spmd, body=%wide.region_37.40_spmd.sunk | while | flops 538443520 | bytes 9861245 | solution.py:67
  255.4 3.4 bitcast_dynamic-update-slice_fusion.16
  259.1 2.1 fusion.241
  261.6 3.3 bitcast_dynamic-update-slice_fusion.16
  267.6 3.3 bitcast_dynamic-update-slice_fusion.16
  273.7 3.3 bitcast_dynamic-update-slice_fusion.16
  280.7 8.8 %all-gather.27 = f32[8,1,128]{2,1,0:T(1,128)S(1)} all-gather(f32[1,1,128]{2,1,0:T(1,128)S(1)} %bitcast.592), channel_id=15, replica_groups=mesh['comp'=8,'samp'=4] {'comp'}, dimensions={0}, use_global_device_ids=true | all-gather | bytes 4608 | tf_op jit(solution)/shard_map/all_gather | solution.py:16
  289.5 7.9 %all-gather.26 = f32[8,1,128]{2,1,0:T(1,128)S(1)} all-gather(f32[1,1,128]{2,1,0:T(1,128)S(1)} %bitcast.586), channel_id=14, replica_groups=mesh['comp'=8,'samp'=4] {'comp'}, dimensions={0}, use_global_device_ids=true | all-gather | bytes 4608 | tf_op jit(solution)/shard_map/all_gather | solution.py:16
  297.4 11.2 %all-gather.45.cloned.1.call-done = f32[1024,512]{1,0:T(8,128)} async-done(((f32[128,512]{1,0:T(8,128)}), f32[1024,512]{1,0:T(8,128)}) %all-gather.45.cloned.1.call-update) | async-done | bytes 2097168 | tf_op jit(solution)/shard_map/all_gather | solution.py:16
  312.5 2.2 broadcast.66
  314.8 24.3 %while.190 = (s32[]{:T(128)}, f32[4,128,2048]{1,2,0:T(8,128)}, f32[4,128]{1,0:T(4,128)S(1)}, f32[4,128]{1,0:T(4,128)S(1)}, f32[4,128,512]{2,1,0:T(8,128)S(1)}, /...) while((s32[]{:T(128)}, f32[4,128,2048]{1,2,0:T(8,128)}, ...), condition=%wide.region_49.50_spmd, body=%wide.region_46.49_spmd.sunk | while | flops 538443520 | bytes 9861245 | solution.py:67
  314.9 3.3 bitcast_dynamic-update-slice_fusion.17
  320.9 3.3 bitcast_dynamic-update-slice_fusion.17
  327.1 3.3 bitcast_dynamic-update-slice_fusion.17
  333.1 3.3 bitcast_dynamic-update-slice_fusion.17
  340.1 4.8 %fusion.144 = (f32[4,2048]{1,0:T(4,128)S(1)}, f32[4,2048]{1,0:T(4,128)S(1)}) fusion(f32[4,128,2048]{1,2,0:T(8,128)} %get-tuple-element.538, f32[128]{0:T(128)S(1)} %get-tuple-element.511, f32[128]{0:T(128)S(1)} %get-tuple-element.539, f32[128]{0:T(128)S(1)} %get-tuple-element.516, f32[4,128,2048]{1,2,0:T(8,128)} %get-tuple-element.540, ...), kind=kLoop, calls=%fused_computation.175 | loop fusion | flops 6275072 | bytes 8456192 | tf_op jit(solution)/shard_map/reduce_sum | solution.py:83
  346.0 2.4 fusion.146
  348.4 8.7 %all-gather.29 = f32[8,1,128]{2,1,0:T(1,128)S(1)} all-gather(f32[1,1,128]{2,1,0:T(1,128)S(1)} %bitcast.587), channel_id=18, replica_groups=mesh['comp'=8,'samp'=4] {'comp'}, dimensions={0}, use_global_device_ids=true | all-gather | bytes 4608 | tf_op jit(solution)/shard_map/all_gather | solution.py:16
  357.1 8.0 %all-gather.28 = f32[8,1,128]{2,1,0:T(1,128)S(1)} all-gather(f32[1,1,128]{2,1,0:T(1,128)S(1)} %bitcast.581), channel_id=17, replica_groups=mesh['comp'=8,'samp'=4] {'comp'}, dimensions={0}, use_global_device_ids=true | all-gather | bytes 4608 | tf_op jit(solution)/shard_map/all_gather | solution.py:16
  365.1 2.9 all-gather.47.cloned.1.call-done
  371.4 4.7 %fusion.148 = (f32[4,2048]{1,0:T(4,128)S(1)}, f32[4,2048]{1,0:T(4,128)S(1)}) fusion(f32[4,128,2048]{1,2,0:T(8,128)} %get-tuple-element.546, f32[128]{0:T(128)S(1)} %get-tuple-element.531, f32[128]{0:T(128)S(1)} %get-tuple-element.547, f32[128]{0:T(128)S(1)} %get-tuple-element.536, f32[4,128,2048]{1,2,0:T(8,128)} %get-tuple-element.548, ...), kind=kLoop, calls=%fused_computation.179 | loop fusion | flops 6275072 | bytes 8456192 | tf_op jit(solution)/shard_map/reduce_sum | solution.py:83
  376.1 19.0 %psum.7 = f32[8192]{0:T(1024)S(1)} all-reduce(f32[8192]{0:T(1024)S(1)} %bitcast.562), channel_id=1, replica_groups=mesh['comp'=8,'samp'=4] {'samp'}, use_global_device_ids=true, to_apply=%region_61.62 | all-reduce | flops 8192 | bytes 65536 | tf_op jit(solution)/shard_map/psum | solution.py:85
  (352 shorter events, 94.3 us)
Async XLA Ops:
  7.2 63.6 %all-gather.37.cloned.1.call-start = ((), (), s32[]{:S(2)}) async-start(), calls=%async_computation | async-start | bytes 2359296 | tf_op jit(solution)/shard_map/all_gather | solution.py:16
  7.2 5.2 %copy-start.3 = (f32[8192]{0:T(1024)S(1)}, f32[8192]{0:T(1024)}, u32[]{:S(2)}) copy-start(f32[8192]{0:T(1024)} %param.30) | copy-start | bytes 98308
  7.2 5.2 %copy-start.2 = (f32[128,512]{1,0:T(8,128)S(1)}, f32[128,512]{1,0:T(8,128)}, u32[]{:S(2)}) copy-start(f32[128,512]{1,0:T(8,128)} %param.28) | copy-start | bytes 786436
  40.1 90.1 %all-gather.39.cloned.1.call-start = ((), (), s32[]{:S(2)}) async-start(), calls=%async_computation.1 | async-start | bytes 2359296 | tf_op jit(solution)/shard_map/all_gather | solution.py:16
  70.7 1.7 slice-start.1
  102.2 87.4 %all-gather.41.cloned.1.call-start = ((), (), s32[]{:S(2)}) async-start(), calls=%async_computation.2 | async-start | bytes 2359296 | tf_op jit(solution)/shard_map/all_gather | solution.py:16
  130.2 1.7 slice-start.2
  161.7 87.4 %all-gather.43.cloned.1.call-start = ((), (), s32[]{:S(2)}) async-start(), calls=%async_computation.3 | async-start | bytes 2359296 | tf_op jit(solution)/shard_map/all_gather | solution.py:16
  189.6 1.7 slice-start.3
  221.2 87.4 %all-gather.45.cloned.1.call-start = ((), (), s32[]{:S(2)}) async-start(), calls=%async_computation.4 | async-start | bytes 2359296 | tf_op jit(solution)/shard_map/all_gather | solution.py:16
  249.1 1.7 slice-start.4
  280.6 87.4 %all-gather.47.cloned.1.call-start = ((), (), s32[]{:S(2)}) async-start(), calls=%async_computation.5 | async-start | bytes 2359296 | tf_op jit(solution)/shard_map/all_gather | solution.py:16
  308.6 1.7 slice-start.5
  340.1 4.8 %copy-start = (f32[4,128,2048]{1,2,0:T(8,128)S(1)}, f32[4,128,2048]{1,2,0:T(8,128)}, u32[]{:S(2)}) copy-start(f32[4,128,2048]{1,2,0:T(8,128)} %get-tuple-element.542) | copy-start | bytes 12582916
  340.1 5.9 %copy-start.1 = (f32[4,128,2048]{1,2,0:T(8,128)S(1)}, f32[4,128,2048]{1,2,0:T(8,128)}, u32[]{:S(2)}) copy-start(f32[4,128,2048]{1,2,0:T(8,128)} %get-tuple-element.544) | copy-start | bytes 12582916
  368.0 1.7 slice-start
Sparse Core Ops, SparseCore 0:
  40.2 30.5 all-gather.36
  102.4 27.7 all-gather.38
  161.8 27.7 all-gather.40
  221.3 27.7 all-gather.42
  280.8 27.7 all-gather.44
  340.2 27.7 all-gather.46
where the time goes:
time: 406 us; the launch traced here: 404 us
  matrix products  130 us (32%)
  blocking collectives  122 us (30%)
  waiting for transfers between devices  59.1 us (15%)
  other arithmetic  50.2 us (12%)
  local copies, waits for them, and re-layouts  27.2 us (7%)
  between operations  14.6 us (4%)
    all_gather x12, blocking collectives, joined(): pieces = jax.tree.map(lambda part: lax.all_gather(part, axis), value)  103 us
    dot_general x24, matrix products, partial_block(): lax.dot_general(points_bf, center_block, (((1,), (1,)), ((), ())), prefer...  79.4 us
    all_gather x6, waiting for transfers between devices, joined(): pieces = jax.tree.map(lambda part: lax.all_gather(part, axis), value)  59 us
    dot_general x24, matrix products, partial_block(): jnp.dot(expd.astype(jnp.bfloat16), center_block, preferred_element_type=j...  50.3 us
    psum x1, blocking collectives, body(): occupancy_all = lax.psum(occupancy_sum, 'samp')  19 us
    another operation x24, local copies, waits for them, and re-layouts  14.1 us
    reduce_sum x3, other arithmetic, body(): occupancy_sum = occupancy_sum + jnp.sum(shares, axis=1).reshape(kdev)  11.8 us
    slice x18, local copies, waits for them, and re-layouts, joined(): tail = jax.tree.map(lambda part: part[1:], pieces)  10.1 us
  transfers between devices with their start and end apart: 6, of which 6 were waited for; matrix products, arithmetic and copies ran while one was open for 2% of the time, Pallas kernels for 0%

commit v1 on v0

v1 whole, which is shorter than its diff:
```python
import functools

import jax
import jax.numpy as jnp
from jax import lax
from jax.experimental import pallas as pl
from jax.experimental.pallas import tpu as pltpu
from jax.sharding import PartitionSpec as P

MESH = pl.DeviceIdType.MESH
LANES = 128
drift_rate = 0.5
noise_gain = 1.0


def lane_tiles(value):
    return [value[:, i : i + LANES] for i in range(0, value.shape[1], LANES)]


def kernel(
    n,
    zn,
    occ_scale,
    chunk,
    start_ref,
    centers_ref,
    lw_ref,
    noise_ref,
    points_out,
    logm_out,
    occ_out,
    cen,
    cent,
    bias,
    sco,
    pull,
    rbuf,
    stat_send,
    stat_buf,
    pts,
    occ,
    occ_buf,
    load_sem,
    rs_send,
    rs_recv,
    st_send,
    st_recv,
    ag_send,
    ag_recv,
    oc_send,
    oc_recv,
):
    rows, width = start_ref.shape
    kdev = centers_ref.shape[0]
    steps = noise_ref.shape[0]
    nchunks = kdev // chunk
    crows, cwidth = rbuf.shape[1], rbuf.shape[2]
    per_row = width // cwidth
    me = lax.axis_index("comp")
    mz = lax.axis_index("samp")

    def part(c):
        r = pl.multiple_of((c // per_row) * crows, crows)
        w = pl.multiple_of((c % per_row) * cwidth, cwidth)
        return pl.ds(r, crows), pl.ds(w, cwidth)

    def load(j):
        blk = pl.ds(j * chunk, chunk)
        return pltpu.make_async_copy(centers_ref.at[blk], cen.at[blk], load_sem.at[j])

    for j in range(nchunks):
        load(j).start()
    barrier = pltpu.get_barrier_semaphore()
    for k in range(1, n):
        pl.semaphore_signal(
            barrier, inc=1, device_id={"comp": lax.rem(me + k, n)}, device_id_type=MESH
        )
    for k in range(1, zn):
        pl.semaphore_signal(
            barrier, inc=1, device_id={"samp": lax.rem(mz + k, zn)}, device_id_type=MESH
        )
    pts[...] = start_ref[...]
    stat_send[...] = jnp.zeros_like(stat_send)
    occ[...] = jnp.zeros_like(occ)

    for j in range(nchunks):
        load(j).wait()
        blk = slice(j * chunk, (j + 1) * chunk)
        turned = cen[blk, :].T
        cent[:, blk] = turned
        wide = turned.astype(jnp.float32)
        bias[:, blk] = lw_ref[:, blk] - 0.5 * jnp.sum(wide * wide, axis=0, keepdims=True)
    pl.semaphore_wait(barrier, n - 1 + zn - 1)

    row_id = lax.broadcasted_iota(jnp.int32, (rows, LANES), 0)
    lane_id = lax.broadcasted_iota(jnp.int32, (rows, LANES), 1)
    eye = row_id == lane_id
    my_rows, my_cols = part(me)
    chunk_row = (
        lax.broadcasted_iota(jnp.int32, (crows, LANES), 0) + (me // per_row) * crows
    )
    chunk_eye = chunk_row == lax.broadcasted_iota(jnp.int32, (crows, LANES), 1)

    def rs_copy(peer_send, peer_recv):
        return pltpu.make_async_remote_copy(
            src_ref=pull.at[part(peer_send)],
            dst_ref=rbuf.at[me if peer_recv is None else peer_recv],
            send_sem=rs_send.at[peer_send],
            recv_sem=rs_recv.at[me if peer_recv is None else peer_recv],
            device_id={"comp": peer_send},
            device_id_type=MESH,
        )

    def st_copy(peer_send, peer_recv):
        slot = me if peer_recv is None else peer_recv
        return pltpu.make_async_remote_copy(
            src_ref=stat_send,
            dst_ref=stat_buf.at[slot],
            send_sem=st_send.at[peer_send],
            recv_sem=st_recv.at[slot],
            device_id={"comp": peer_send},
            device_id_type=MESH,
        )

    def ag_copy(peer_send, peer_recv):
        slot = me if peer_recv is None else peer_recv
        return pltpu.make_async_remote_copy(
            src_ref=pts.at[my_rows, my_cols],
            dst_ref=pts.at[part(slot)],
            send_sem=ag_send.at[peer_send],
            recv_sem=ag_recv.at[slot],
            device_id={"comp": peer_send},
            device_id_type=MESH,
        )

    def step(t, carry):
        points_bf = pts[...].astype(jnp.bfloat16)
        best = None
        for j in range(nchunks):
            blk = slice(j * chunk, (j + 1) * chunk)
            s = jnp.dot(points_bf, cent[:, blk], preferred_element_type=jnp.float32)
            s = s + bias[:, blk]
            sco[:, blk] = s
            local = functools.reduce(jnp.maximum, lane_tiles(s))
            best = local if best is None else jnp.maximum(best, local)
        top = jnp.max(best, axis=1, keepdims=True)
        mass = None
        acc = None
        for j in range(nchunks):
            blk = slice(j * chunk, (j + 1) * chunk)
            e = jnp.exp(sco[:, blk] - top)
            sco[:, blk] = e
            local = functools.reduce(jnp.add, lane_tiles(e))
            mass = local if mass is None else mass + local
            d = jnp.dot(
                e.astype(jnp.bfloat16), cen[blk, :], preferred_element_type=jnp.float32
            )
            acc = d if acc is None else acc + d
        pull[...] = acc
        total = jnp.sum(mass, axis=1, keepdims=True)
        stat_send[0:1, :] = jnp.sum(jnp.where(eye, top, 0.0), axis=0, keepdims=True)
        stat_send[1:2, :] = jnp.sum(jnp.where(eye, total, 0.0), axis=0, keepdims=True)
        for k in range(1, n):
            st_copy(lax.rem(me + k, n), None).start()
        for k in range(1, n):
            rs_copy(lax.rem(me + k, n), None).start()
        stat_buf[me] = stat_send[...]
        for k in range(1, n):
            st_copy(lax.rem(me + k, n), lax.rem(me + n - k, n)).wait_recv()

        tops = [stat_buf[d, 0:1, :] for d in range(n)]
        row_top = functools.reduce(jnp.maximum, tops)
        total_mass = functools.reduce(
            jnp.add,
            [jnp.exp(tops[d] - row_top) * stat_buf[d, 1:2, :] for d in range(n)],
        )
        logm_out[...] = row_top + jnp.log(total_mass)

        def gain(d):
            return jnp.exp(stat_buf[d, 0:1, :] - row_top) / total_mass

        def chunk_gain(d):
            return jnp.sum(jnp.where(chunk_eye, gain(d), 0.0), axis=1, keepdims=True)

        mine = pull[my_rows, my_cols] * chunk_gain(me)
        share = jnp.sum(jnp.where(eye, gain(me), 0.0), axis=1, keepdims=True)
        gains = [chunk_gain(lax.rem(me + n - k, n)) for k in range(1, n)]
        for k in range(1, n):
            src = lax.rem(me + n - k, n)
            rs_copy(lax.rem(me + k, n), src).wait_recv()
            mine = mine + rbuf[src] * gains[k - 1]
        pts[my_rows, my_cols] = (
            (1.0 - drift_rate) * pts[my_rows, my_cols]
            + drift_rate * mine
            + noise_gain * noise_ref[t, my_rows, my_cols].astype(jnp.float32)
        )
        for k in range(1, n):
            ag_copy(lax.rem(me + k, n), None).start()
        for j in range(nchunks):
            blk = slice(j * chunk, (j + 1) * chunk)
            o = sco[:, blk] * share
            occ[:, blk] += jnp.sum(o.reshape(rows // 8, 8, chunk), axis=0)
        for k in range(1, n):
            to, src = lax.rem(me + k, n), lax.rem(me + n - k, n)
            ag_copy(to, src).wait_recv()
            st_copy(to, src).wait_send()
            rs_copy(to, src).wait_send()
            ag_copy(to, src).wait_send()
        return carry

    lax.fori_loop(0, steps, step, 0)

    occ_buf[mz] = jnp.sum(occ[...], axis=0, keepdims=True)

    def oc_copy(to, slot):
        return pltpu.make_async_remote_copy(
            src_ref=occ_buf.at[mz],
            dst_ref=occ_buf.at[slot],
            send_sem=oc_send.at[to],
            recv_sem=oc_recv.at[slot],
            device_id={"samp": to},
            device_id_type=MESH,
        )

    for k in range(1, zn):
        oc_copy(lax.rem(mz + k, zn), mz).start()
    points_out[...] = pts[...]
    for k in range(1, zn):
        oc_copy(lax.rem(mz + k, zn), lax.rem(mz + zn - k, zn)).wait()
    occ_out[...] = functools.reduce(jnp.add, [occ_buf[d] for d in range(zn)]) * occ_scale


def body(n, zn, start_points, centers, log_weights, noise_draws):
    rows, width = start_points.shape
    kdev = centers.shape[0]
    steps = noise_draws.shape[0]
    crows = max(8, rows // n)
    cwidth = rows * width // (n * crows)
    chunk = min(1024, kdev)
    nchunks = kdev // chunk
    occ_scale = (kdev * n) / (rows * zn * steps)
    f32 = jnp.float32
    vmem = pl.BlockSpec(memory_space=pltpu.VMEM)
    dma = pltpu.SemaphoreType.DMA
    points, logm, occ = pl.pallas_call(
        functools.partial(kernel, n, zn, occ_scale, chunk),
        out_shape=(
            jax.ShapeDtypeStruct((rows, width), f32),
            jax.ShapeDtypeStruct((1, rows), f32),
            jax.ShapeDtypeStruct((1, kdev), f32),
        ),
        in_specs=[vmem, pl.BlockSpec(memory_space=pl.ANY), vmem, vmem],
        out_specs=(vmem, vmem, vmem),
        scratch_shapes=[
            pltpu.VMEM((kdev, width), jnp.bfloat16),
            pltpu.VMEM((width, kdev), jnp.bfloat16),
            pltpu.VMEM((1, kdev), f32),
            pltpu.VMEM((rows, kdev), f32),
            pltpu.VMEM((rows, width), f32),
            pltpu.VMEM((n, crows, cwidth), f32),
            pltpu.VMEM((8, rows), f32),
            pltpu.VMEM((n, 8, rows), f32),
            pltpu.VMEM((rows, width), f32),
            pltpu.VMEM((8, kdev), f32),
            pltpu.VMEM((zn, 1, kdev), f32),
            dma((nchunks,)),
            dma((n,)),
            dma((n,)),
            dma((n,)),
            dma((n,)),
            dma((n,)),
            dma((n,)),
            dma((zn,)),
            dma((zn,)),
        ],
        compiler_params=pltpu.CompilerParams(
            collective_id=0, has_side_effects=True, vmem_limit_bytes=60 * 1024 * 1024
        ),
    )(start_points, centers, log_weights.reshape(1, kdev), noise_draws)
    return points, logm.reshape(rows), occ.reshape(kdev)


def solution(mesh):
    n, zn = mesh.shape["comp"], mesh.shape["samp"]
    return jax.shard_map(
        functools.partial(body, n, zn),
        mesh=mesh,
        in_specs=(P("samp", None), P("comp", None), P("comp"), P(None, "samp", None)),
        out_specs=(P("samp", None), P("samp"), P("comp")),
        check_vma=False,
    )
```

time: 406 us -> 97.1 us (0.24)
  matrix products: 130 us -> 0 us
  blocking collectives: 122 us -> 0 us
  Pallas kernels: 0 us -> 92 us
  waiting for transfers between devices: 59.1 us -> 0 us
  other arithmetic: 50.2 us -> 0 us
  local copies, waits for them, and re-layouts: 27.2 us -> 4.23 us
  between operations: 14.6 us -> 0.64 us
    dot_general x48 -> x0, matrix products: 130 us -> none  [the longest x24 79.4 us: partial_block(): lax.dot_general(points_bf, center_block, (((1,), (1,)), ((), ())), prefer...]
    all_gather x12 -> x0, blocking collectives: 103 us -> none  [joined(): pieces = jax.tree.map(lambda part: lax.all_gather(part, axis), value)]
    pallas_call x0 -> x1, Pallas kernels: none -> 92 us  [body(): pl.pallas_call(functools.partial(kernel, n, zn, occ_scale, chunk), out_sh...]
    all_gather x6 -> x0, waiting for transfers between devices: 59 us -> none  [joined(): pieces = jax.tree.map(lambda part: lax.all_gather(part, axis), value)]
    reduce_sum x40 -> x0, other arithmetic: 29.2 us -> none  [the longest x3 11.8 us: body(): occupancy_sum = occupancy_sum + jnp.sum(shares, axis=1).reshape(kdev)]
    psum x1 -> x0, blocking collectives: 19 us -> none  [body(): occupancy_all = lax.psum(occupancy_sum, 'samp')]
    another operation x24 -> x0, local copies, waits for them, and re-layouts: 14.1 us -> none
    slice x42 -> x0, local copies, waits for them, and re-layouts: 10.2 us -> none  [the longest x18 10.1 us: joined(): tail = jax.tree.map(lambda part: part[1:], pieces)]
  transfers between devices with their start and end apart: 6 -> 0, of which waited for: 6 -> 0; matrix products, arithmetic and copies ran while one was open for 2% -> 0% of each run, Pallas kernels for 0% -> 0%
where the time goes in v1:
time: 97.1 us; the launch traced here: 96.8 us
  Pallas kernels  92 us (95%)
  local copies, waits for them, and re-layouts  4.23 us (4%)
    pallas_call x1, Pallas kernels, body(): pl.pallas_call(functools.partial(kernel, n, zn, occ_scale, chunk), out_sh...  92 us
    unnamed x3, local copies, waits for them, and re-layouts  4.23 us

profile of v1, /device:TPU:0, one launch (start us, length us, event | category | flops | bytes accessed | tf_op | source)
XLA Modules:
  0.0 96.8 jit_solution(6082880063441208501)
XLA Ops:
  0.6 92.0 %shard_map.67 = (f32[128,512]{1,0:T(8,128)}, f32[1,128]{1,0:T(1,128)}, f32[1,8192]{1,0:T(1,128)}) custom-call(f32[128,512]{1,0:T(8,128)} %start_ref.1, bf16[8192,512]{1,0:T(8,128)(2,1)} %centers_ref.1, f32[1,8192]{1,0:T(1,128)} %bitcast.3, bf16[6,128,512]{2,1,0:T(8,128)(2,1)} %noise_ref.1), custom_call_target="tpu_custom_call" | custom-call | tf_op jit(solution)/shard_map/pallas_call | solution.py:245
  92.6 1.7 %copy.10 = f32[128,512]{1,0:T(8,128)} copy(f32[128,512]{1,0:T(8,128)} %get-tuple-element.12) | data formatting | bytes 524288
  94.3 1.2 %copy.11 = f32[128]{0:T(128)} copy(f32[128]{0:T(128)} %bitcast.5) | data formatting | bytes 1024
  95.5 1.4 %copy.12 = f32[8192]{0:T(1024)} copy(f32[8192]{0:T(1024)} %bitcast.4) | data formatting | bytes 65536
